TPU v7x, 32 devices: a whole 2x2x4 slice. The times are simulated.
32 devices in a mesh: seq: 4 (over x, core), ctx: 4 (over z), head: 2 (over y).
Axes of the slice: x: 2, y: 2, z: 4, core: 2. Of those that a mesh axis runs over, the one named last changes fastest.
Arguments:
- stream: bfloat16 [4, 256, 2880], P('seq', 'ctx'), may hold values from -6 to 6
- query_weight: bfloat16 [2880, 4096], P(None, 'head'), may hold values from -0.109375 to 0.109375
- cache_keys: bfloat16 [4, 8192, 8, 64], P('seq', 'ctx', 'head'), may hold values from -1000 to 1000
- cache_values: bfloat16 [4, 8192, 8, 64], P('seq', 'ctx', 'head'), may hold values from -6 to 6
- new_keys: bfloat16 [4, 256, 8, 64], P('seq', 'ctx', 'head'), may hold values from -18 to 18
- new_values: bfloat16 [4, 256, 8, 64], P('seq', 'ctx', 'head'), may hold values from -6 to 6
- out_weight: bfloat16 [4096, 2880], P('head'), may hold values from -0.09375 to 0.09375
- norm_gain: float32 [2880], replicated, may hold values from 0.5 to 1.5
- expert_ids: int32 [4, 256, 4], P('seq', 'ctx'), may hold values from 0 to 15, all different within a row; in each aligned block of 64 rows (0 to 63, 64 to 127, ..., all dimensions but the last counted through in order) at most 16 rows name the same one
- expert_weights: float32 [4, 256, 4], P('seq', 'ctx'), may hold values from 0.1 to 1
- gate_weight: bfloat16 [16, 2880, 2880], P(('seq', 'ctx'), None, 'head'), may hold values from -0.109375 to 0.109375
- up_weight: bfloat16 [16, 2880, 2880], P(('seq', 'ctx'), None, 'head'), may hold values from -0.109375 to 0.109375
- down_weight: bfloat16 [16, 2880, 2880], P(('seq', 'ctx'), 'head'), may hold values from -0.109375 to 0.109375
Outputs:
- mixed: bfloat16 [4, 256, 2880], P('seq', 'ctx', 'head')
Inputs may be any that keep to these rules, and one draw needn't show every extreme that they name: `expert_ids`: in each aligned block of 64 rows (the tokens of one device) no expert is named by more than 16 rows; each row names 4 different experts.
All inputs are finite; a program needn't handle non-finite values.
Results may differ from a plain program's by a relative error of at most 0.015.
Values may be sent and summed in bfloat16 or wider, within the bound.
No kernel may reach another device: no remote copies, remote signals or barrier semaphores. Data moves between devices by JAX's collectives and lax.ppermute only.
A program may use at most 128 MiB of HBM per device.

v0:
```python
import math
import jax
import jax.numpy as jnp
from jax import lax
from jax.sharding import PartitionSpec as P

CAP = 16


def passed_along(block, axis, distance):
    devices = range(lax.axis_size(axis))
    route = [((i - distance) % len(devices), i) for i in devices]
    return lax.ppermute(block, axis, route)


def body(
    stream,
    query_weight,
    cache_keys,
    cache_values,
    new_keys,
    new_values,
    out_weight,
    norm_gain,
    expert_ids,
    expert_weights,
    gate_weight,
    up_weight,
    down_weight,
):
    tokens = stream[0]
    count = tokens.shape[0]
    model = tokens.shape[1]
    kv_local = cache_keys.shape[2]
    head_dim = cache_keys.shape[3]
    group = query_weight.shape[1] // (kv_local * head_dim)
    cache_len = cache_keys.shape[1]
    height = count * group
    cycles = lax.axis_size("ctx")
    place = lax.axis_index("ctx")
    scale = 1.0 / math.sqrt(head_dim)
    query = jnp.dot(tokens, query_weight, preferred_element_type=jnp.float32).astype(jnp.bfloat16)
    query = (
        query.reshape(count, kv_local, group, head_dim)
        .transpose(1, 0, 2, 3)
        .reshape(kv_local, height, head_dim)
    )
    keys = jnp.concatenate([cache_keys[0], new_keys[0]], axis=0).transpose(1, 0, 2)
    values = jnp.concatenate([cache_values[0], new_values[0]], axis=0).transpose(1, 0, 2)
    extent = keys.shape[1]
    key_index = lax.broadcasted_iota(jnp.int32, (height, extent), 1)
    tok_index = lax.broadcasted_iota(jnp.int32, (height, extent), 0) // group
    fresh = key_index - cache_len
    blank = (
        jnp.full((kv_local, height), -jnp.inf, jnp.float32),
        jnp.zeros((kv_local, height), jnp.float32),
        jnp.zeros((kv_local, height, head_dim), jnp.float32),
    )

    def absorb(block, state, sources):
        top, total, numerator = state
        anchor = sources[:, None]
        allowed = (
            (key_index < cache_len) | (place < anchor) | (place == anchor) & (fresh <= tok_index)
        )
        scores = jnp.einsum("hrd,hkd->hrk", block, keys, preferred_element_type=jnp.float32) * scale
        scores = jnp.where(allowed[None], scores, -jnp.inf)
        new_top = jnp.maximum(top, jnp.max(scores, axis=-1))
        weights = jnp.exp(scores - new_top[..., None])
        fade = jnp.exp(top - new_top)
        total = total * fade + jnp.sum(weights, axis=-1)
        numerator = numerator * fade[..., None] + jnp.einsum(
            "hrk,hkd->hrd", weights.astype(jnp.bfloat16), values, preferred_element_type=jnp.float32
        )
        return (new_top, total, numerator)

    def turn(step, carry):
        sources = jnp.full((height,), (place - step) % cycles, jnp.int32)
        state = absorb(carry[0].astype(jnp.bfloat16), carry[1:], sources)
        return passed_along((carry[0],) + state, "ctx", 1)

    final = lax.fori_loop(0, cycles, turn, (query.astype(jnp.float32),) + blank)
    top, total, numerator = (final[1], final[2], final[3])
    attn = (numerator / total[..., None]).astype(jnp.bfloat16)
    attn = (
        attn.reshape(kv_local, count, group, head_dim)
        .transpose(1, 0, 2, 3)
        .reshape(count, kv_local * group * head_dim)
    )
    projected = jnp.dot(attn, out_weight, preferred_element_type=jnp.float32)
    width = model // lax.axis_size("head")
    offset = lax.axis_index("head") * width
    resid = tokens.astype(jnp.float32) + lax.psum(projected.astype(jnp.bfloat16), "head").astype(
        jnp.float32
    )
    normed = (
        resid * lax.rsqrt(jnp.mean(resid * resid, axis=-1, keepdims=True) + 1e-05) * norm_gain
    ).astype(jnp.bfloat16)
    resid_own = lax.dynamic_slice_in_dim(resid, offset, width, 1)
    experts = lax.axis_size("seq") * lax.axis_size("ctx")
    slots = experts * CAP
    chosen = expert_ids[0].reshape(-1)
    onehot = (chosen[:, None] == lax.broadcasted_iota(jnp.int32, (1, experts), 1)).astype(jnp.int32)
    before = jnp.cumsum(onehot, axis=0) - onehot
    target = chosen * CAP + jnp.sum(before * onehot, axis=1)
    matches = target[None, :] == lax.broadcasted_iota(jnp.int32, (slots, 1), 0)
    select = jnp.sum(matches.astype(jnp.float32).reshape(slots, count, -1), axis=-1).astype(
        jnp.bfloat16
    )
    packed = jnp.dot(select, normed, preferred_element_type=jnp.float32).astype(jnp.bfloat16)
    packed = packed.reshape(experts, CAP, normed.shape[1])
    arrived = lax.all_to_all(packed, ("seq", "ctx"), split_axis=0, concat_axis=0, tiled=True)
    rows = arrived.reshape(slots, normed.shape[1])
    gate = jnp.dot(rows, gate_weight[0], preferred_element_type=jnp.float32)
    up = jnp.dot(rows, up_weight[0], preferred_element_type=jnp.float32)
    hidden = (gate * jax.nn.sigmoid(1.702 * gate) * (up + 1.0)).astype(jnp.bfloat16)
    columns = down_weight[0]
    expert_out = lax.psum_scatter(
        jnp.einsum("fd,rf->dr", columns, hidden, preferred_element_type=jnp.float32).astype(
            jnp.bfloat16
        ),
        "head",
        scatter_dimension=0,
        tiled=True,
    )
    returned = lax.all_to_all(expert_out, ("seq", "ctx"), split_axis=1, concat_axis=1, tiled=True)
    spread_weights = jnp.where(matches.T, expert_weights[0].reshape(-1)[:, None], 0.0)
    spread_weights = jnp.sum(spread_weights.reshape(count, -1, slots), axis=1)
    moe = lax.dot_general(
        spread_weights,
        returned.astype(jnp.float32),
        (((1,), (1,)), ((), ())),
        precision=lax.Precision.HIGHEST,
    )
    return (resid_own + moe).astype(jnp.bfloat16)[None]


def solution(mesh):
    in_specs = (
        P("seq", "ctx", None),
        P(None, "head"),
        P("seq", "ctx", "head", None),
        P("seq", "ctx", "head", None),
        P("seq", "ctx", "head", None),
        P("seq", "ctx", "head", None),
        P("head", None),
        P(),
        P("seq", "ctx", None),
        P("seq", "ctx", None),
        P(("seq", "ctx"), None, "head"),
        P(("seq", "ctx"), None, "head"),
        P(("seq", "ctx"), "head", None),
    )
    out_specs = P("seq", "ctx", "head")
    return jax.shard_map(body, mesh=mesh, in_specs=in_specs, out_specs=out_specs, check_vma=False)
```

profile of v0, /device:TPU:0, one launch (start us, length us, event | category | flops | bytes accessed | tf_op | source)
XLA Modules:
  0.0 386.5 jit_solution(13312295736175083786)
XLA Ops:
  6.6 0.9 copy.34
  7.5 0.9 copy.35
  8.5 6.7 %fusion.43 = bf16[64,2048]{1,0:T(8,128)(2,1)S(1)} fusion(bf16[2880,2048]{1,0:T(8,128)(2,1)} %param.16, bf16[1,64,2880]{2,1,0:T(8,128)(2,1)} %param.15), kind=kOutput, calls=%fused_computation.38 | convolution fusion | flops 755105792 | bytes 12427264 | tf_op jit(solution)/shard_map/dot_general | solution.py:42
  15.2 0.5 reshape.177
  15.7 0.1 copy.50
  15.8 0.2 copy.36
  16.0 0.4 copy-done.2
  16.4 2.4 maximum_bitcast_fusion
  18.9 205.2 %while.22 = (s32[]{:T(128)}, bf16[4,512,64]{1,2,0:T(8,128)(2,1)S(1)}, f32[4,512]{1,0:T(4,128)S(1)}, f32[4,512]{1,0:T(4,128)S(1)}, f32[4,512,64]{1,2,0:T(8,128)S(...) while((s32[]{:T(128)}, ...), condition=%wide.region_3.4_spmd.clone, body=%wide.region_0.3_spmd.clone.sunk | while | flops 1161629696 | bytes 63567040 | solution.py:82
  19.1 1.3 fusion.86
  20.5 7.7 %fusion.87 = (f32[4,512]{1,0:T(4,128)S(1)}, f32[4,512,2112]{1,2,0:T(8,128)}) fusion(pred[512,2112]{0,1:T(8,128)(4,1)S(1)} %fusion.86, bf16[4,512,64]{1,2,0:T(8,128)(2,1)S(1)} %copy.57, bf16[4,2112,64]{1,2,0:T(8,128)(2,1)S(1)} %get-tuple-element.480), kind=kOutput, calls=%fused_computation.4.clone.1 | convolution fusion | flops 566622208 | bytes 19734528 | tf_op jit(solution)/shard_map/while/body/eval_jaxpr/hrd,hkd->hrk/dot_general | solution.py:66
  28.2 9.6 %fusion.88 = f32[4,512]{1,0:T(4,128)S(1)} fusion(f32[4,512,2112]{1,2,0:T(8,128)} %get-tuple-element.439, f32[4,512]{1,0:T(4,128)S(1)} %max.12, pred[512,2112]{0,1:T(8,128)(4,1)S(1)} %fusion.86), kind=kLoop, calls=%fused_computation.6.clone.1 | loop fusion | flops 17299456 | bytes 18399232 | tf_op jit(solution)/shard_map/while/body/eval_jaxpr/reduce_sum | solution.py:71
  37.8 11.6 %fusion.89 = f32[4,512,64]{1,2,0:T(8,128)} fusion(bf16[4,2112,64]{1,2,0:T(8,128)(2,1)} %get-tuple-element.481, f32[4,512,2112]{1,2,0:T(8,128)} %get-tuple-element.439, f32[4,512]{1,0:T(4,128)S(1)} %max.12, pred[512,2112]{0,1:T(8,128)(4,1)S(1)} %fusion.86, f32[4,512,64]{1,2,0:T(8,128)S(1)} %get-tuple-element.462, f32[4,512]{1,0:T(4,128)S(1)} %get-tuple-element.441), kind=kOutput, calls=%fused_computation.15.clone.1 | convolution fusion | flops 571211776 | bytes 20529152 | tf_op jit(solution)/shard_map/while/body/eval_jaxpr/hrk,hkd->hrd/dot_general | solution.py:72
  49.4 3.1 collective-permute-start.3
  52.4 1.6 collective-permute-start
  54.0 1.6 collective-permute-start.1
  55.6 16.9 %collective-permute-done.1 = f32[4,512]{1,0:T(4,128)S(1)} collective-permute-done((f32[4,512]{1,0:T(4,128)S(1)}, f32[4,512]{1,0:T(4,128)S(1)}, u32[]{:S(2)}, u32[]{:S(2)}) %collective-permute-start.1) | collective-permute-done | bytes 8224 | tf_op jit(solution)/shard_map/while/body/eval_jaxpr/ppermute | solution.py:13
  72.6 1.3 fusion.86
  73.9 7.7 %fusion.87 = (f32[4,512]{1,0:T(4,128)S(1)}, f32[4,512,2112]{1,2,0:T(8,128)}) fusion(pred[512,2112]{0,1:T(8,128)(4,1)S(1)} %fusion.86, bf16[4,512,64]{1,2,0:T(8,128)(2,1)S(1)} %copy.57, bf16[4,2112,64]{1,2,0:T(8,128)(2,1)S(1)} %get-tuple-element.480), kind=kOutput, calls=%fused_computation.4.clone.1 | convolution fusion | flops 566622208 | bytes 19734528 | tf_op jit(solution)/shard_map/while/body/eval_jaxpr/hrd,hkd->hrk/dot_general | solution.py:66
  81.6 9.6 %fusion.88 = f32[4,512]{1,0:T(4,128)S(1)} fusion(f32[4,512,2112]{1,2,0:T(8,128)} %get-tuple-element.439, f32[4,512]{1,0:T(4,128)S(1)} %max.12, pred[512,2112]{0,1:T(8,128)(4,1)S(1)} %fusion.86), kind=kLoop, calls=%fused_computation.6.clone.1 | loop fusion | flops 17299456 | bytes 18399232 | tf_op jit(solution)/shard_map/while/body/eval_jaxpr/reduce_sum | solution.py:71
  91.2 11.6 %fusion.89 = f32[4,512,64]{1,2,0:T(8,128)} fusion(bf16[4,2112,64]{1,2,0:T(8,128)(2,1)} %get-tuple-element.481, f32[4,512,2112]{1,2,0:T(8,128)} %get-tuple-element.439, f32[4,512]{1,0:T(4,128)S(1)} %max.12, pred[512,2112]{0,1:T(8,128)(4,1)S(1)} %fusion.86, f32[4,512,64]{1,2,0:T(8,128)S(1)} %get-tuple-element.462, f32[4,512]{1,0:T(4,128)S(1)} %get-tuple-element.441), kind=kOutput, calls=%fused_computation.15.clone.1 | convolution fusion | flops 571211776 | bytes 20529152 | tf_op jit(solution)/shard_map/while/body/eval_jaxpr/hrk,hkd->hrd/dot_general | solution.py:72
  102.8 1.3 collective-permute-start
  104.1 1.6 collective-permute-start.1
  105.7 2.1 collective-permute-start.2
  107.8 16.0 %collective-permute-done.1 = f32[4,512]{1,0:T(4,128)S(1)} collective-permute-done((f32[4,512]{1,0:T(4,128)S(1)}, f32[4,512]{1,0:T(4,128)S(1)}, u32[]{:S(2)}, u32[]{:S(2)}) %collective-permute-start.1) | collective-permute-done | bytes 8224 | tf_op jit(solution)/shard_map/while/body/eval_jaxpr/ppermute | solution.py:13
  123.9 1.3 fusion.86
  125.2 7.7 %fusion.87 = (f32[4,512]{1,0:T(4,128)S(1)}, f32[4,512,2112]{1,2,0:T(8,128)}) fusion(pred[512,2112]{0,1:T(8,128)(4,1)S(1)} %fusion.86, bf16[4,512,64]{1,2,0:T(8,128)(2,1)S(1)} %copy.57, bf16[4,2112,64]{1,2,0:T(8,128)(2,1)S(1)} %get-tuple-element.480), kind=kOutput, calls=%fused_computation.4.clone.1 | convolution fusion | flops 566622208 | bytes 19734528 | tf_op jit(solution)/shard_map/while/body/eval_jaxpr/hrd,hkd->hrk/dot_general | solution.py:66
  133.0 9.6 %fusion.88 = f32[4,512]{1,0:T(4,128)S(1)} fusion(f32[4,512,2112]{1,2,0:T(8,128)} %get-tuple-element.439, f32[4,512]{1,0:T(4,128)S(1)} %max.12, pred[512,2112]{0,1:T(8,128)(4,1)S(1)} %fusion.86), kind=kLoop, calls=%fused_computation.6.clone.1 | loop fusion | flops 17299456 | bytes 18399232 | tf_op jit(solution)/shard_map/while/body/eval_jaxpr/reduce_sum | solution.py:71
  142.5 11.6 %fusion.89 = f32[4,512,64]{1,2,0:T(8,128)} fusion(bf16[4,2112,64]{1,2,0:T(8,128)(2,1)} %get-tuple-element.481, f32[4,512,2112]{1,2,0:T(8,128)} %get-tuple-element.439, f32[4,512]{1,0:T(4,128)S(1)} %max.12, pred[512,2112]{0,1:T(8,128)(4,1)S(1)} %fusion.86, f32[4,512,64]{1,2,0:T(8,128)S(1)} %get-tuple-element.462, f32[4,512]{1,0:T(4,128)S(1)} %get-tuple-element.441), kind=kOutput, calls=%fused_computation.15.clone.1 | convolution fusion | flops 571211776 | bytes 20529152 | tf_op jit(solution)/shard_map/while/body/eval_jaxpr/hrk,hkd->hrd/dot_general | solution.py:72
  154.1 0.8 collective-permute-start.1
  154.9 4.2 %collective-permute-start.2 = (f32[4,512]{1,0:T(4,128)S(1)}, f32[4,512]{1,0:T(4,128)S(1)}, u32[]{:S(2)}, u32[]{:S(2)}) collective-permute-start(f32[4,512]{1,0:T(4,128)S(1)} %get-tuple-element.440), channel_id=1, source_target_pairs={{6,0},{0,2},{2,4},{4,6},{7,1},{1,3},{3,5},{5,7},{14,8},{8,10},{10,... | collective-permute-start | bytes 24584 | tf_op jit(solution)/shard_map/while/body/eval_jaxpr/ppermute | solution.py:13
  159.1 15.2 %collective-permute-done.1 = f32[4,512]{1,0:T(4,128)S(1)} collective-permute-done((f32[4,512]{1,0:T(4,128)S(1)}, f32[4,512]{1,0:T(4,128)S(1)}, u32[]{:S(2)}, u32[]{:S(2)}) %collective-permute-start.1) | collective-permute-done | bytes 8224 | tf_op jit(solution)/shard_map/while/body/eval_jaxpr/ppermute | solution.py:13
  174.4 1.3 fusion.86
  175.7 7.7 %fusion.87 = (f32[4,512]{1,0:T(4,128)S(1)}, f32[4,512,2112]{1,2,0:T(8,128)}) fusion(pred[512,2112]{0,1:T(8,128)(4,1)S(1)} %fusion.86, bf16[4,512,64]{1,2,0:T(8,128)(2,1)S(1)} %copy.57, bf16[4,2112,64]{1,2,0:T(8,128)(2,1)S(1)} %get-tuple-element.480), kind=kOutput, calls=%fused_computation.4.clone.1 | convolution fusion | flops 566622208 | bytes 19734528 | tf_op jit(solution)/shard_map/while/body/eval_jaxpr/hrd,hkd->hrk/dot_general | solution.py:66
  183.4 9.6 %fusion.88 = f32[4,512]{1,0:T(4,128)S(1)} fusion(f32[4,512,2112]{1,2,0:T(8,128)} %get-tuple-element.439, f32[4,512]{1,0:T(4,128)S(1)} %max.12, pred[512,2112]{0,1:T(8,128)(4,1)S(1)} %fusion.86), kind=kLoop, calls=%fused_computation.6.clone.1 | loop fusion | flops 17299456 | bytes 18399232 | tf_op jit(solution)/shard_map/while/body/eval_jaxpr/reduce_sum | solution.py:71
  193.0 11.6 %fusion.89 = f32[4,512,64]{1,2,0:T(8,128)} fusion(bf16[4,2112,64]{1,2,0:T(8,128)(2,1)} %get-tuple-element.481, f32[4,512,2112]{1,2,0:T(8,128)} %get-tuple-element.439, f32[4,512]{1,0:T(4,128)S(1)} %max.12, pred[512,2112]{0,1:T(8,128)(4,1)S(1)} %fusion.86, f32[4,512,64]{1,2,0:T(8,128)S(1)} %get-tuple-element.462, f32[4,512]{1,0:T(4,128)S(1)} %get-tuple-element.441), kind=kOutput, calls=%fused_computation.15.clone.1 | convolution fusion | flops 571211776 | bytes 20529152 | tf_op jit(solution)/shard_map/while/body/eval_jaxpr/hrk,hkd->hrd/dot_general | solution.py:72
  204.6 0.7 collective-permute-start.1
  205.3 4.3 %collective-permute-start.2 = (f32[4,512]{1,0:T(4,128)S(1)}, f32[4,512]{1,0:T(4,128)S(1)}, u32[]{:S(2)}, u32[]{:S(2)}) collective-permute-start(f32[4,512]{1,0:T(4,128)S(1)} %get-tuple-element.440), channel_id=1, source_target_pairs={{6,0},{0,2},{2,4},{4,6},{7,1},{1,3},{3,5},{5,7},{14,8},{8,10},{10,... | collective-permute-start | bytes 24584 | tf_op jit(solution)/shard_map/while/body/eval_jaxpr/ppermute | solution.py:13
  209.5 14.3 %collective-permute-done.1 = f32[4,512]{1,0:T(4,128)S(1)} collective-permute-done((f32[4,512]{1,0:T(4,128)S(1)}, f32[4,512]{1,0:T(4,128)S(1)}, u32[]{:S(2)}, u32[]{:S(2)}) %collective-permute-start.1) | collective-permute-done | bytes 8224 | tf_op jit(solution)/shard_map/while/body/eval_jaxpr/ppermute | solution.py:13
  224.1 0.3 copy.37
  224.5 0.3 fusion.49
  224.8 0.1 copy.38
  224.9 0.5 reshape.172
  225.4 8.8 %convolution_convert_fusion.1 = bf16[64,2880]{1,0:T(8,128)(2,1)} fusion(bf16[64,2048]{1,0:T(8,128)(2,1)S(1)} %reshape.172, bf16[2048,2880]{0,1:T(8,128)(2,1)} %param.21), kind=kOutput, calls=%fused_computation.31 | convolution fusion | flops 755159040 | bytes 12427264 | tf_op jit(solution)/shard_map/dot_general | solution.py:90
  234.3 0.1 copy.39
  234.4 0.1 eq.71
  234.5 0.1 eq.67
  234.6 0.6 reduce-window.6
  235.2 0.2 slice_reduce_fusion
  235.5 0.1 reduce_sum.55
  235.7 0.1 convert_reduce_fusion
  235.8 21.4 %all-reduce.2.cloned.1.call-done = bf16[64,2880]{1,0:T(8,128)(2,1)} async-done(((bf16[64,2880]{1,0:T(8,128)(2,1)}), bf16[64,2880]{1,0:T(8,128)(2,1)}) %all-reduce.2.cloned.1.call-update) | async-done | bytes 368656 | tf_op jit(solution)/shard_map/psum | solution.py:93
  257.3 2.1 convert_add_fusion
  259.4 1.7 convolution_convert_fusion
  261.1 1.0 copy.45
  262.1 42.1 %all_to_all.17 = bf16[16,16,2880]{2,1,0:T(8,128)(2,1)S(1)} all-to-all(bf16[16,16,2880]{2,1,0:T(8,128)(2,1)S(1)} %bitcast.102), channel_id=1, replica_groups=mesh['seq'=4,'ctx'=4,'head'=2] {'seq','ctx'}, dimensions={0} | all-to-all | bytes 2949120 | tf_op jit(solution)/shard_map/all_to_all | solution.py:112
  304.1 5.9 %fusion.25 = f32[256,1440]{0,1:T(8,128)S(1)} fusion(bf16[256,2880]{1,0:T(8,128)(2,1)S(1)} %bitcast.105, bf16[1,2880,1440]{1,2,0:T(8,128)(2,1)} %param.25), kind=kOutput, calls=%fused_computation.26 | convolution fusion | flops 2123366400 | bytes 11243520 | tf_op jit(solution)/shard_map/dot_general | solution.py:114
  310.0 16.2 %fusion.30 = bf16[2880,256]{1,0:T(8,128)(2,1)} fusion(bf16[1,1440,2880]{2,1,0:T(8,128)(2,1)} %param.27, bf16[256,2880]{1,0:T(8,128)(2,1)S(1)} %bitcast.106, bf16[1,2880,1440]{1,2,0:T(8,128)(2,1)} %param.26, f32[256,1440]{0,1:T(8,128)S(1)} %fusion.25), kind=kOutput, calls=%fused_computation.30 | convolution fusion | flops 4250419200 | bytes 21012480 | tf_op jit(solution)/shard_map/fd,rf->dr/dot_general | solution.py:119
  326.3 23.0 %reduce-scatter.2.cloned.1.call-done = bf16[1440,256]{1,0:T(8,128)(2,1)} async-done(((bf16[2880,256]{1,0:T(8,128)(2,1)}), bf16[1440,256]{1,0:T(8,128)(2,1)}) %reduce-scatter.2.cloned.1.call-update) | async-done | bytes 737296 | tf_op jit(solution)/shard_map/reduce_scatter | solution.py:118
  349.3 2.3 copy.46
  351.6 5.6 %all-to-all-start.1 = ((bf16[1440,16,16]{0,2,1:T(8,128)(2,1)}), bf16[1440,16,16]{0,2,1:T(8,128)(2,1)S(1)}, u32[]{:S(2)}, u32[]{:S(2)}) async-start(bf16[1440,16,16]{0,2,1:T(8,128)(2,1)} %bitcast.20), calls=%async_computation.2 | async-start | bytes 1572864 | tf_op jit(solution)/shard_map/all_to_all | solution.py:126
  357.2 0.1 select_reduce_fusion
  357.4 21.1 %all-to-all-done.1 = bf16[1440,16,16]{0,2,1:T(8,128)(2,1)S(1)} async-done(((bf16[1440,16,16]{0,2,1:T(8,128)(2,1)}), bf16[1440,16,16]{0,2,1:T(8,128)(2,1)S(1)}, u32[]{:S(2)}, u32[]{:S(2)}) %all-to-all-start.1) | async-done | bytes 737312 | tf_op jit(solution)/shard_map/all_to_all | solution.py:126
  378.4 1.2 fusion.44
  (58 shorter events, 1.0 us)
Async XLA Ops:
  6.5 250.7 %all-reduce.2.cloned.1.call-start = ((), (), s32[]{:S(2)}) async-start(), calls=%async_computation.3 | async-start | bytes 753664 | tf_op jit(solution)/shard_map/psum | solution.py:93
  15.2 1.2 copy-start.2
  49.4 23.2 %collective-permute-start.3 = (f32[4,512,64]{1,2,0:T(8,128)}, f32[4,512,64]{1,2,0:T(8,128)S(1)}, u32[]{:S(2)}, u32[]{:S(2)}) collective-permute-start(f32[4,512,64]{1,2,0:T(8,128)} %fusion.89), channel_id=1, source_target_pairs={{6,0},{0,2},{2,4},{4,6},{7,1},{1,3},{3,5},{5,7},{14,8},{8,10},{10,... | collective-permute-start | bytes 1572872 | tf_op jit(solution)/shard_map/while/body/eval_jaxpr/ppermute | solution.py:13
  52.4 20.1 %collective-permute-start = (bf16[4,512,64]{1,2,0:T(8,128)(2,1)S(1)}, bf16[4,512,64]{1,2,0:T(8,128)(2,1)S(1)}, u32[]{:S(2)}, u32[]{:S(2)}) collective-permute-start(bf16[4,512,64]{1,2,0:T(8,128)(2,1)S(1)} %copy.57), channel_id=1, source_target_pairs={{6,0},{0,2},{2,4},{4,6},{7,1},{1,3},{3,5},{5,7},{14,8},{8,10},{10,... | collective-permute-start | bytes 786440 | tf_op jit(solution)/shard_map/while/body/eval_jaxpr/ppermute | solution.py:13
  54.0 18.5 %collective-permute-start.1 = (f32[4,512]{1,0:T(4,128)S(1)}, f32[4,512]{1,0:T(4,128)S(1)}, u32[]{:S(2)}, u32[]{:S(2)}) collective-permute-start(f32[4,512]{1,0:T(4,128)S(1)} %max.12), channel_id=1, source_target_pairs={{6,0},{0,2},{2,4},{4,6},{7,1},{1,3},{3,5},{5,7},{14,8},{8,10},{10,... | collective-permute-start | bytes 24584 | tf_op jit(solution)/shard_map/while/body/eval_jaxpr/ppermute | solution.py:13
  55.6 17.0 %collective-permute-start.2 = (f32[4,512]{1,0:T(4,128)S(1)}, f32[4,512]{1,0:T(4,128)S(1)}, u32[]{:S(2)}, u32[]{:S(2)}) collective-permute-start(f32[4,512]{1,0:T(4,128)S(1)} %get-tuple-element.440), channel_id=1, source_target_pairs={{6,0},{0,2},{2,4},{4,6},{7,1},{1,3},{3,5},{5,7},{14,8},{8,10},{10,... | collective-permute-start | bytes 24584 | tf_op jit(solution)/shard_map/while/body/eval_jaxpr/ppermute | solution.py:13
  102.8 21.1 %collective-permute-start.3 = (f32[4,512,64]{1,2,0:T(8,128)}, f32[4,512,64]{1,2,0:T(8,128)S(1)}, u32[]{:S(2)}, u32[]{:S(2)}) collective-permute-start(f32[4,512,64]{1,2,0:T(8,128)} %fusion.89), channel_id=1, source_target_pairs={{6,0},{0,2},{2,4},{4,6},{7,1},{1,3},{3,5},{5,7},{14,8},{8,10},{10,... | collective-permute-start | bytes 1572872 | tf_op jit(solution)/shard_map/while/body/eval_jaxpr/ppermute | solution.py:13
  102.8 21.1 %collective-permute-start = (bf16[4,512,64]{1,2,0:T(8,128)(2,1)S(1)}, bf16[4,512,64]{1,2,0:T(8,128)(2,1)S(1)}, u32[]{:S(2)}, u32[]{:S(2)}) collective-permute-start(bf16[4,512,64]{1,2,0:T(8,128)(2,1)S(1)} %copy.57), channel_id=1, source_target_pairs={{6,0},{0,2},{2,4},{4,6},{7,1},{1,3},{3,5},{5,7},{14,8},{8,10},{10,... | collective-permute-start | bytes 786440 | tf_op jit(solution)/shard_map/while/body/eval_jaxpr/ppermute | solution.py:13
  104.1 19.7 %collective-permute-start.1 = (f32[4,512]{1,0:T(4,128)S(1)}, f32[4,512]{1,0:T(4,128)S(1)}, u32[]{:S(2)}, u32[]{:S(2)}) collective-permute-start(f32[4,512]{1,0:T(4,128)S(1)} %max.12), channel_id=1, source_target_pairs={{6,0},{0,2},{2,4},{4,6},{7,1},{1,3},{3,5},{5,7},{14,8},{8,10},{10,... | collective-permute-start | bytes 24584 | tf_op jit(solution)/shard_map/while/body/eval_jaxpr/ppermute | solution.py:13
  105.7 18.2 %collective-permute-start.2 = (f32[4,512]{1,0:T(4,128)S(1)}, f32[4,512]{1,0:T(4,128)S(1)}, u32[]{:S(2)}, u32[]{:S(2)}) collective-permute-start(f32[4,512]{1,0:T(4,128)S(1)} %get-tuple-element.440), channel_id=1, source_target_pairs={{6,0},{0,2},{2,4},{4,6},{7,1},{1,3},{3,5},{5,7},{14,8},{8,10},{10,... | collective-permute-start | bytes 24584 | tf_op jit(solution)/shard_map/while/body/eval_jaxpr/ppermute | solution.py:13
  154.1 20.2 %collective-permute-start.3 = (f32[4,512,64]{1,2,0:T(8,128)}, f32[4,512,64]{1,2,0:T(8,128)S(1)}, u32[]{:S(2)}, u32[]{:S(2)}) collective-permute-start(f32[4,512,64]{1,2,0:T(8,128)} %fusion.89), channel_id=1, source_target_pairs={{6,0},{0,2},{2,4},{4,6},{7,1},{1,3},{3,5},{5,7},{14,8},{8,10},{10,... | collective-permute-start | bytes 1572872 | tf_op jit(solution)/shard_map/while/body/eval_jaxpr/ppermute | solution.py:13
  154.1 20.2 %collective-permute-start = (bf16[4,512,64]{1,2,0:T(8,128)(2,1)S(1)}, bf16[4,512,64]{1,2,0:T(8,128)(2,1)S(1)}, u32[]{:S(2)}, u32[]{:S(2)}) collective-permute-start(bf16[4,512,64]{1,2,0:T(8,128)(2,1)S(1)} %copy.57), channel_id=1, source_target_pairs={{6,0},{0,2},{2,4},{4,6},{7,1},{1,3},{3,5},{5,7},{14,8},{8,10},{10,... | collective-permute-start | bytes 786440 | tf_op jit(solution)/shard_map/while/body/eval_jaxpr/ppermute | solution.py:13
  154.1 20.1 %collective-permute-start.1 = (f32[4,512]{1,0:T(4,128)S(1)}, f32[4,512]{1,0:T(4,128)S(1)}, u32[]{:S(2)}, u32[]{:S(2)}) collective-permute-start(f32[4,512]{1,0:T(4,128)S(1)} %max.12), channel_id=1, source_target_pairs={{6,0},{0,2},{2,4},{4,6},{7,1},{1,3},{3,5},{5,7},{14,8},{8,10},{10,... | collective-permute-start | bytes 24584 | tf_op jit(solution)/shard_map/while/body/eval_jaxpr/ppermute | solution.py:13
  154.9 19.4 %collective-permute-start.2 = (f32[4,512]{1,0:T(4,128)S(1)}, f32[4,512]{1,0:T(4,128)S(1)}, u32[]{:S(2)}, u32[]{:S(2)}) collective-permute-start(f32[4,512]{1,0:T(4,128)S(1)} %get-tuple-element.440), channel_id=1, source_target_pairs={{6,0},{0,2},{2,4},{4,6},{7,1},{1,3},{3,5},{5,7},{14,8},{8,10},{10,... | collective-permute-start | bytes 24584 | tf_op jit(solution)/shard_map/while/body/eval_jaxpr/ppermute | solution.py:13
  204.6 19.4 %collective-permute-start.3 = (f32[4,512,64]{1,2,0:T(8,128)}, f32[4,512,64]{1,2,0:T(8,128)S(1)}, u32[]{:S(2)}, u32[]{:S(2)}) collective-permute-start(f32[4,512,64]{1,2,0:T(8,128)} %fusion.89), channel_id=1, source_target_pairs={{6,0},{0,2},{2,4},{4,6},{7,1},{1,3},{3,5},{5,7},{14,8},{8,10},{10,... | collective-permute-start | bytes 1572872 | tf_op jit(solution)/shard_map/while/body/eval_jaxpr/ppermute | solution.py:13
  204.6 19.4 %collective-permute-start = (bf16[4,512,64]{1,2,0:T(8,128)(2,1)S(1)}, bf16[4,512,64]{1,2,0:T(8,128)(2,1)S(1)}, u32[]{:S(2)}, u32[]{:S(2)}) collective-permute-start(bf16[4,512,64]{1,2,0:T(8,128)(2,1)S(1)} %copy.57), channel_id=1, source_target_pairs={{6,0},{0,2},{2,4},{4,6},{7,1},{1,3},{3,5},{5,7},{14,8},{8,10},{10,... | collective-permute-start | bytes 786440 | tf_op jit(solution)/shard_map/while/body/eval_jaxpr/ppermute | solution.py:13
  204.6 19.3 %collective-permute-start.1 = (f32[4,512]{1,0:T(4,128)S(1)}, f32[4,512]{1,0:T(4,128)S(1)}, u32[]{:S(2)}, u32[]{:S(2)}) collective-permute-start(f32[4,512]{1,0:T(4,128)S(1)} %max.12), channel_id=1, source_target_pairs={{6,0},{0,2},{2,4},{4,6},{7,1},{1,3},{3,5},{5,7},{14,8},{8,10},{10,... | collective-permute-start | bytes 24584 | tf_op jit(solution)/shard_map/while/body/eval_jaxpr/ppermute | solution.py:13
  205.3 18.7 %collective-permute-start.2 = (f32[4,512]{1,0:T(4,128)S(1)}, f32[4,512]{1,0:T(4,128)S(1)}, u32[]{:S(2)}, u32[]{:S(2)}) collective-permute-start(f32[4,512]{1,0:T(4,128)S(1)} %get-tuple-element.440), channel_id=1, source_target_pairs={{6,0},{0,2},{2,4},{4,6},{7,1},{1,3},{3,5},{5,7},{14,8},{8,10},{10,... | collective-permute-start | bytes 24584 | tf_op jit(solution)/shard_map/while/body/eval_jaxpr/ppermute | solution.py:13
  225.4 8.9 %copy-start.4 = (s32[1,64,4]{1,2,0:T(4,128)S(1)}, s32[1,64,4]{1,2,0:T(4,128)}, u32[]{:S(2)}) copy-start(s32[1,64,4]{1,2,0:T(4,128)} %param.23) | copy-start | bytes 3076
  225.4 31.9 %copy-start = (bf16[1,64,2880]{2,1,0:T(8,128)(2,1)S(1)}, bf16[1,64,2880]{2,1,0:T(8,128)(2,1)}, u32[]{:S(2)}) copy-start(bf16[1,64,2880]{2,1,0:T(8,128)(2,1)} %param.15) | copy-start | bytes 1105924
  234.2 25.2 %copy-start.3 = (f32[2880]{0:T(1024)S(1)}, f32[2880]{0:T(1024)}, u32[]{:S(2)}) copy-start(f32[2880]{0:T(1024)} %param.22) | copy-start | bytes 34564
  234.2 115.1 %reduce-scatter.2.cloned.1.call-start = ((), (), s32[]{:S(2)}) async-start(), calls=%async_computation.4 | async-start | bytes 2211840 | tf_op jit(solution)/shard_map/reduce_scatter | solution.py:118
  326.3 30.9 %copy-start.5 = (f32[1,64,4]{1,2,0:T(4,128)S(1)}, f32[1,64,4]{1,2,0:T(4,128)}, u32[]{:S(2)}) copy-start(f32[1,64,4]{1,2,0:T(4,128)} %param.24) | copy-start | bytes 3076
  326.3 52.2 %copy-start.1 = (f32[64,2880]{1,0:T(8,128)S(1)}, f32[64,2880]{1,0:T(8,128)}, u32[]{:S(2)}) copy-start(f32[64,2880]{1,0:T(8,128)} %get-tuple-element.355) | copy-start | bytes 2211844
  351.6 26.8 %all-to-all-start.1 = ((bf16[1440,16,16]{0,2,1:T(8,128)(2,1)}), bf16[1440,16,16]{0,2,1:T(8,128)(2,1)S(1)}, u32[]{:S(2)}, u32[]{:S(2)}) async-start(bf16[1440,16,16]{0,2,1:T(8,128)(2,1)} %bitcast.20), calls=%async_computation.2 | async-start | bytes 1572864 | tf_op jit(solution)/shard_map/all_to_all | solution.py:126
Sparse Core Ops, SparseCore 0:
  234.3 22.8 all-reduce.1
  326.4 22.8 reduce-scatter.1
where the time goes:
time: 387 us; the launch traced here: 386 us
  waiting for transfers between devices  128 us (33%)
  matrix products  118 us (30%)
  other arithmetic  49.5 us (13%)
  blocking collectives  42.1 us (11%)
  starting transfers between devices  26.7 us (7%)
  between operations  13.6 us (4%)
  local copies, waits for them, and re-layouts  8.03 us (2%)
    ppermute x16, waiting for transfers between devices, passed_along(): return lax.ppermute(block, axis, route)  62.7 us
    dot_general x4, matrix products, absorb(): jnp.einsum('hrk,hkd->hrd', weights.astype(jnp.bfloat16), values, preferre...  46.3 us
    all_to_all x1, blocking collectives, body(): lax.all_to_all(packed, ('seq', 'ctx'), split_axis=0, concat_axis=0, tiled...  42.1 us
    reduce_sum x4, other arithmetic, absorb(): total = total * fade + jnp.sum(weights, axis=-1)  38.2 us
    dot_general x4, matrix products, absorb(): jnp.einsum('hrd,hkd->hrk', block, keys, preferred_element_type=jnp.float32)  30.9 us
    reduce_scatter x1, waiting for transfers between devices, body(): lax.psum_scatter(jnp.einsum('fd,rf->dr', columns, hidden, preferred_eleme...  23 us
    psum x1, waiting for transfers between devices, body(): lax.psum(projected.astype(jnp.bfloat16), 'head').astype(jnp.float32)  21.4 us
    ppermute x16, starting transfers between devices, passed_along(): return lax.ppermute(block, axis, route)  21.1 us
  transfers between devices with their start and end apart: 19, of which 11 were waited for; matrix products, arithmetic and copies ran while one was open for 0% of the time, Pallas kernels for 0%

commit v1 on v0

--- a/solution.py
+++ b/solution.py
@@ -123,7 +123,9 @@
         scatter_dimension=0,
         tiled=True,
     )
-    returned = lax.all_to_all(expert_out, ("seq", "ctx"), split_axis=1, concat_axis=1, tiled=True)
+    pieces = jnp.split(expert_out, lax.axis_size(("seq", "ctx")), axis=1)
+    received = lax.all_to_all(jnp.stack(pieces), ("seq", "ctx"), 0, 0)
+    returned = jnp.concatenate(received, axis=1)
     spread_weights = jnp.where(matches.T, expert_weights[0].reshape(-1)[:, None], 0.0)
     spread_weights = jnp.sum(spread_weights.reshape(count, -1, slots), axis=1)
     moe = lax.dot_general(

time: 387 us -> 417 us (1.078)
  local copies, waits for them, and re-layouts: 8.03 us -> 37 us
    another operation x1 -> x19, local copies, waits for them, and re-layouts: 0.01 us -> 18.8 us  [the longest x18 18.8 us: body(): received = lax.all_to_all(jnp.stack(pieces), ('seq', 'ctx'), 0, 0)]
    unnamed x16 -> x31, local copies, waits for them, and re-layouts: 2.6 us -> 15.1 us
where the time goes in v1:
time: 417 us; the launch traced here: 415 us
  waiting for transfers between devices  128 us (31%)
  matrix products  118 us (28%)
  other arithmetic  49.5 us (12%)
  blocking collectives  42.1 us (10%)
  local copies, waits for them, and re-layouts  37 us (9%)
  starting transfers between devices  26.7 us (6%)
  between operations  13.7 us (3%)
    ppermute x16, waiting for transfers between devices, passed_along(): return lax.ppermute(block, axis, route)  62.7 us
    dot_general x4, matrix products, absorb(): jnp.einsum('hrk,hkd->hrd', weights.astype(jnp.bfloat16), values, preferre...  46.3 us
    all_to_all x1, blocking collectives, body(): lax.all_to_all(packed, ('seq', 'ctx'), split_axis=0, concat_axis=0, tiled...  42.1 us
    reduce_sum x4, other arithmetic, absorb(): total = total * fade + jnp.sum(weights, axis=-1)  38.2 us
    dot_general x4, matrix products, absorb(): jnp.einsum('hrd,hkd->hrk', block, keys, preferred_element_type=jnp.float32)  30.9 us
    reduce_scatter x1, waiting for transfers between devices, body(): lax.psum_scatter(jnp.einsum('fd,rf->dr', columns, hidden, preferred_eleme...  23 us
    psum x1, waiting for transfers between devices, body(): lax.psum(projected.astype(jnp.bfloat16), 'head').astype(jnp.float32)  21.4 us
    ppermute x16, starting transfers between devices, passed_along(): return lax.ppermute(block, axis, route)  21.1 us
  transfers between devices with their start and end apart: 19, of which 11 were waited for; matrix products, arithmetic and copies ran while one was open for 0% of the time, Pallas kernels for 0%

profile of v1, /device:TPU:0, one launch (start us, length us, event | category | flops | bytes accessed | tf_op | source)
XLA Modules:
  0.0 415.5 jit_solution(11660024576236889951)
XLA Ops:
  6.6 0.9 copy.62
  7.5 0.9 copy.63
  8.5 6.7 %fusion.43 = bf16[64,2048]{1,0:T(8,128)(2,1)S(1)} fusion(bf16[2880,2048]{1,0:T(8,128)(2,1)} %param.16, bf16[1,64,2880]{2,1,0:T(8,128)(2,1)} %param.15), kind=kOutput, calls=%fused_computation.38 | convolution fusion | flops 755105792 | bytes 12427264 | tf_op jit(solution)/shard_map/dot_general | solution.py:42
  16.4 2.4 maximum_bitcast_fusion
  18.9 205.2 %while.22 = (s32[]{:T(128)}, bf16[4,512,64]{1,2,0:T(8,128)(2,1)S(1)}, f32[4,512]{1,0:T(4,128)S(1)}, f32[4,512]{1,0:T(4,128)S(1)}, f32[4,512,64]{1,2,0:T(8,128)S(...) while((s32[]{:T(128)}, ...), condition=%wide.region_3.4_spmd.clone, body=%wide.region_0.3_spmd.clone.sunk | while | flops 1161629696 | bytes 63567040 | solution.py:82
  19.1 1.3 fusion.86
  20.5 7.7 %fusion.87 = (f32[4,512]{1,0:T(4,128)S(1)}, f32[4,512,2112]{1,2,0:T(8,128)}) fusion(pred[512,2112]{0,1:T(8,128)(4,1)S(1)} %fusion.86, bf16[4,512,64]{1,2,0:T(8,128)(2,1)S(1)} %copy.100, bf16[4,2112,64]{1,2,0:T(8,128)(2,1)S(1)} %get-tuple-element.508), kind=kOutput, calls=%fused_computation.4.clone.1 | convolution fusion | flops 566622208 | bytes 19734528 | tf_op jit(solution)/shard_map/while/body/eval_jaxpr/hrd,hkd->hrk/dot_general | solution.py:66
  28.2 9.6 %fusion.88 = f32[4,512]{1,0:T(4,128)S(1)} fusion(f32[4,512,2112]{1,2,0:T(8,128)} %get-tuple-element.467, f32[4,512]{1,0:T(4,128)S(1)} %max.12, pred[512,2112]{0,1:T(8,128)(4,1)S(1)} %fusion.86), kind=kLoop, calls=%fused_computation.6.clone.1 | loop fusion | flops 17299456 | bytes 18399232 | tf_op jit(solution)/shard_map/while/body/eval_jaxpr/reduce_sum | solution.py:71
  37.8 11.6 %fusion.89 = f32[4,512,64]{1,2,0:T(8,128)} fusion(bf16[4,2112,64]{1,2,0:T(8,128)(2,1)} %get-tuple-element.509, f32[4,512,2112]{1,2,0:T(8,128)} %get-tuple-element.467, f32[4,512]{1,0:T(4,128)S(1)} %max.12, pred[512,2112]{0,1:T(8,128)(4,1)S(1)} %fusion.86, f32[4,512,64]{1,2,0:T(8,128)S(1)} %get-tuple-element.490, f32[4,512]{1,0:T(4,128)S(1)} %get-tuple-element.469), kind=kOutput, calls=%fused_computation.15.clone.1 | convolution fusion | flops 571211776 | bytes 20529152 | tf_op jit(solution)/shard_map/while/body/eval_jaxpr/hrk,hkd->hrd/dot_general | solution.py:72
  49.4 3.1 collective-permute-start.3
  52.4 1.6 collective-permute-start
  54.0 1.6 collective-permute-start.1
  55.6 16.9 %collective-permute-done.1 = f32[4,512]{1,0:T(4,128)S(1)} collective-permute-done((f32[4,512]{1,0:T(4,128)S(1)}, f32[4,512]{1,0:T(4,128)S(1)}, u32[]{:S(2)}, u32[]{:S(2)}) %collective-permute-start.1) | collective-permute-done | bytes 8224 | tf_op jit(solution)/shard_map/while/body/eval_jaxpr/ppermute | solution.py:13
  72.6 1.3 fusion.86
  73.9 7.7 %fusion.87 = (f32[4,512]{1,0:T(4,128)S(1)}, f32[4,512,2112]{1,2,0:T(8,128)}) fusion(pred[512,2112]{0,1:T(8,128)(4,1)S(1)} %fusion.86, bf16[4,512,64]{1,2,0:T(8,128)(2,1)S(1)} %copy.100, bf16[4,2112,64]{1,2,0:T(8,128)(2,1)S(1)} %get-tuple-element.508), kind=kOutput, calls=%fused_computation.4.clone.1 | convolution fusion | flops 566622208 | bytes 19734528 | tf_op jit(solution)/shard_map/while/body/eval_jaxpr/hrd,hkd->hrk/dot_general | solution.py:66
  81.6 9.6 %fusion.88 = f32[4,512]{1,0:T(4,128)S(1)} fusion(f32[4,512,2112]{1,2,0:T(8,128)} %get-tuple-element.467, f32[4,512]{1,0:T(4,128)S(1)} %max.12, pred[512,2112]{0,1:T(8,128)(4,1)S(1)} %fusion.86), kind=kLoop, calls=%fused_computation.6.clone.1 | loop fusion | flops 17299456 | bytes 18399232 | tf_op jit(solution)/shard_map/while/body/eval_jaxpr/reduce_sum | solution.py:71
  91.2 11.6 %fusion.89 = f32[4,512,64]{1,2,0:T(8,128)} fusion(bf16[4,2112,64]{1,2,0:T(8,128)(2,1)} %get-tuple-element.509, f32[4,512,2112]{1,2,0:T(8,128)} %get-tuple-element.467, f32[4,512]{1,0:T(4,128)S(1)} %max.12, pred[512,2112]{0,1:T(8,128)(4,1)S(1)} %fusion.86, f32[4,512,64]{1,2,0:T(8,128)S(1)} %get-tuple-element.490, f32[4,512]{1,0:T(4,128)S(1)} %get-tuple-element.469), kind=kOutput, calls=%fused_computation.15.clone.1 | convolution fusion | flops 571211776 | bytes 20529152 | tf_op jit(solution)/shard_map/while/body/eval_jaxpr/hrk,hkd->hrd/dot_general | solution.py:72
  102.8 1.3 collective-permute-start
  104.1 1.6 collective-permute-start.1
  105.7 2.1 collective-permute-start.2
  107.8 16.0 %collective-permute-done.1 = f32[4,512]{1,0:T(4,128)S(1)} collective-permute-done((f32[4,512]{1,0:T(4,128)S(1)}, f32[4,512]{1,0:T(4,128)S(1)}, u32[]{:S(2)}, u32[]{:S(2)}) %collective-permute-start.1) | collective-permute-done | bytes 8224 | tf_op jit(solution)/shard_map/while/body/eval_jaxpr/ppermute | solution.py:13
  123.9 1.3 fusion.86
  125.2 7.7 %fusion.87 = (f32[4,512]{1,0:T(4,128)S(1)}, f32[4,512,2112]{1,2,0:T(8,128)}) fusion(pred[512,2112]{0,1:T(8,128)(4,1)S(1)} %fusion.86, bf16[4,512,64]{1,2,0:T(8,128)(2,1)S(1)} %copy.100, bf16[4,2112,64]{1,2,0:T(8,128)(2,1)S(1)} %get-tuple-element.508), kind=kOutput, calls=%fused_computation.4.clone.1 | convolution fusion | flops 566622208 | bytes 19734528 | tf_op jit(solution)/shard_map/while/body/eval_jaxpr/hrd,hkd->hrk/dot_general | solution.py:66
  133.0 9.6 %fusion.88 = f32[4,512]{1,0:T(4,128)S(1)} fusion(f32[4,512,2112]{1,2,0:T(8,128)} %get-tuple-element.467, f32[4,512]{1,0:T(4,128)S(1)} %max.12, pred[512,2112]{0,1:T(8,128)(4,1)S(1)} %fusion.86), kind=kLoop, calls=%fused_computation.6.clone.1 | loop fusion | flops 17299456 | bytes 18399232 | tf_op jit(solution)/shard_map/while/body/eval_jaxpr/reduce_sum | solution.py:71
  142.5 11.6 %fusion.89 = f32[4,512,64]{1,2,0:T(8,128)} fusion(bf16[4,2112,64]{1,2,0:T(8,128)(2,1)} %get-tuple-element.509, f32[4,512,2112]{1,2,0:T(8,128)} %get-tuple-element.467, f32[4,512]{1,0:T(4,128)S(1)} %max.12, pred[512,2112]{0,1:T(8,128)(4,1)S(1)} %fusion.86, f32[4,512,64]{1,2,0:T(8,128)S(1)} %get-tuple-element.490, f32[4,512]{1,0:T(4,128)S(1)} %get-tuple-element.469), kind=kOutput, calls=%fused_computation.15.clone.1 | convolution fusion | flops 571211776 | bytes 20529152 | tf_op jit(solution)/shard_map/while/body/eval_jaxpr/hrk,hkd->hrd/dot_general | solution.py:72
  154.1 0.8 collective-permute-start.1
  154.9 4.2 %collective-permute-start.2 = (f32[4,512]{1,0:T(4,128)S(1)}, f32[4,512]{1,0:T(4,128)S(1)}, u32[]{:S(2)}, u32[]{:S(2)}) collective-permute-start(f32[4,512]{1,0:T(4,128)S(1)} %get-tuple-element.468), channel_id=1, source_target_pairs={{6,0},{0,2},{2,4},{4,6},{7,1},{1,3},{3,5},{5,7},{14,8},{8,10},{10,... | collective-permute-start | bytes 24584 | tf_op jit(solution)/shard_map/while/body/eval_jaxpr/ppermute | solution.py:13
  159.1 15.2 %collective-permute-done.1 = f32[4,512]{1,0:T(4,128)S(1)} collective-permute-done((f32[4,512]{1,0:T(4,128)S(1)}, f32[4,512]{1,0:T(4,128)S(1)}, u32[]{:S(2)}, u32[]{:S(2)}) %collective-permute-start.1) | collective-permute-done | bytes 8224 | tf_op jit(solution)/shard_map/while/body/eval_jaxpr/ppermute | solution.py:13
  174.4 1.3 fusion.86
  175.7 7.7 %fusion.87 = (f32[4,512]{1,0:T(4,128)S(1)}, f32[4,512,2112]{1,2,0:T(8,128)}) fusion(pred[512,2112]{0,1:T(8,128)(4,1)S(1)} %fusion.86, bf16[4,512,64]{1,2,0:T(8,128)(2,1)S(1)} %copy.100, bf16[4,2112,64]{1,2,0:T(8,128)(2,1)S(1)} %get-tuple-element.508), kind=kOutput, calls=%fused_computation.4.clone.1 | convolution fusion | flops 566622208 | bytes 19734528 | tf_op jit(solution)/shard_map/while/body/eval_jaxpr/hrd,hkd->hrk/dot_general | solution.py:66
  183.4 9.6 %fusion.88 = f32[4,512]{1,0:T(4,128)S(1)} fusion(f32[4,512,2112]{1,2,0:T(8,128)} %get-tuple-element.467, f32[4,512]{1,0:T(4,128)S(1)} %max.12, pred[512,2112]{0,1:T(8,128)(4,1)S(1)} %fusion.86), kind=kLoop, calls=%fused_computation.6.clone.1 | loop fusion | flops 17299456 | bytes 18399232 | tf_op jit(solution)/shard_map/while/body/eval_jaxpr/reduce_sum | solution.py:71
  193.0 11.6 %fusion.89 = f32[4,512,64]{1,2,0:T(8,128)} fusion(bf16[4,2112,64]{1,2,0:T(8,128)(2,1)} %get-tuple-element.509, f32[4,512,2112]{1,2,0:T(8,128)} %get-tuple-element.467, f32[4,512]{1,0:T(4,128)S(1)} %max.12, pred[512,2112]{0,1:T(8,128)(4,1)S(1)} %fusion.86, f32[4,512,64]{1,2,0:T(8,128)S(1)} %get-tuple-element.490, f32[4,512]{1,0:T(4,128)S(1)} %get-tuple-element.469), kind=kOutput, calls=%fused_computation.15.clone.1 | convolution fusion | flops 571211776 | bytes 20529152 | tf_op jit(solution)/shard_map/while/body/eval_jaxpr/hrk,hkd->hrd/dot_general | solution.py:72
  204.6 0.7 collective-permute-start.1
  205.3 4.3 %collective-permute-start.2 = (f32[4,512]{1,0:T(4,128)S(1)}, f32[4,512]{1,0:T(4,128)S(1)}, u32[]{:S(2)}, u32[]{:S(2)}) collective-permute-start(f32[4,512]{1,0:T(4,128)S(1)} %get-tuple-element.468), channel_id=1, source_target_pairs={{6,0},{0,2},{2,4},{4,6},{7,1},{1,3},{3,5},{5,7},{14,8},{8,10},{10,... | collective-permute-start | bytes 24584 | tf_op jit(solution)/shard_map/while/body/eval_jaxpr/ppermute | solution.py:13
  209.5 14.3 %collective-permute-done.1 = f32[4,512]{1,0:T(4,128)S(1)} collective-permute-done((f32[4,512]{1,0:T(4,128)S(1)}, f32[4,512]{1,0:T(4,128)S(1)}, u32[]{:S(2)}, u32[]{:S(2)}) %collective-permute-start.1) | collective-permute-done | bytes 8224 | tf_op jit(solution)/shard_map/while/body/eval_jaxpr/ppermute | solution.py:13
  225.4 8.8 %convolution_convert_fusion.1 = bf16[64,2880]{1,0:T(8,128)(2,1)} fusion(bf16[64,2048]{1,0:T(8,128)(2,1)S(1)} %reshape.176, bf16[2048,2880]{0,1:T(8,128)(2,1)} %param.21), kind=kOutput, calls=%fused_computation.31 | convolution fusion | flops 755159040 | bytes 12427264 | tf_op jit(solution)/shard_map/dot_general | solution.py:90
  235.8 21.4 %all-reduce.2.cloned.1.call-done = bf16[64,2880]{1,0:T(8,128)(2,1)} async-done(((bf16[64,2880]{1,0:T(8,128)(2,1)}), bf16[64,2880]{1,0:T(8,128)(2,1)}) %all-reduce.2.cloned.1.call-update) | async-done | bytes 368656 | tf_op jit(solution)/shard_map/psum | solution.py:93
  257.3 2.1 convert_add_fusion
  259.4 1.7 convolution_convert_fusion
  261.1 1.0 copy.73
  262.1 42.1 %all_to_all.10 = bf16[16,16,2880]{2,1,0:T(8,128)(2,1)S(1)} all-to-all(bf16[16,16,2880]{2,1,0:T(8,128)(2,1)S(1)} %bitcast.135), channel_id=1, replica_groups=mesh['seq'=4,'ctx'=4,'head'=2] {'seq','ctx'}, dimensions={0} | all-to-all | bytes 2949120 | tf_op jit(solution)/shard_map/all_to_all | solution.py:112
  304.1 5.9 %fusion.25 = f32[256,1440]{0,1:T(8,128)S(1)} fusion(bf16[256,2880]{1,0:T(8,128)(2,1)S(1)} %bitcast.138, bf16[1,2880,1440]{1,2,0:T(8,128)(2,1)} %param.25), kind=kOutput, calls=%fused_computation.26 | convolution fusion | flops 2123366400 | bytes 11243520 | tf_op jit(solution)/shard_map/dot_general | solution.py:114
  310.0 16.2 %fusion.30 = bf16[2880,256]{1,0:T(8,128)(2,1)} fusion(bf16[1,1440,2880]{2,1,0:T(8,128)(2,1)} %param.27, bf16[256,2880]{1,0:T(8,128)(2,1)S(1)} %bitcast.139, bf16[1,2880,1440]{1,2,0:T(8,128)(2,1)} %param.26, f32[256,1440]{0,1:T(8,128)S(1)} %fusion.25), kind=kOutput, calls=%fused_computation.30 | convolution fusion | flops 4250419200 | bytes 21012480 | tf_op jit(solution)/shard_map/fd,rf->dr/dot_general | solution.py:119
  326.3 23.0 %reduce-scatter.2.cloned.1.call-done = bf16[1440,256]{1,0:T(8,128)(2,1)} async-done(((bf16[2880,256]{1,0:T(8,128)(2,1)}), bf16[1440,256]{1,0:T(8,128)(2,1)}) %reduce-scatter.2.cloned.1.call-update) | async-done | bytes 737296 | tf_op jit(solution)/shard_map/reduce_scatter | solution.py:118
  349.3 6.4 %slice_bitcast_fusion = (bf16[1,1440,16]{2,1,0:T(8,128)(2,1)S(1)}, bf16[1,1440,16]{2,1,0:T(8,128)(2,1)S(1)}, bf16[1,1440,16]{2,1,0:T(8,128)(2,1)S(1)}, bf16[1,14...) fusion(bf16[1440,256]{1,0:T(8,128)(2,1)} %reduce-scatter.2.clon, ...), kind=kLoop, calls=%fused_computation.53 | loop fusion | bytes 1474560 | tf_op jit(solution)/shard_map/stack | solution.py:127
  355.7 1.1 copy.74
  356.9 0.6 constant_dynamic-update-slice_fusion.15
  357.5 1.7 copy.75
  359.2 1.7 copy.76
  361.0 1.7 copy.77
  362.7 1.7 copy.78
  364.5 1.1 copy.79
  365.6 1.1 copy.80
  368.1 1.4 constant_dynamic-update-slice_fusion.14
  369.5 1.4 constant_dynamic-update-slice_fusion.13
  371.0 1.4 constant_dynamic-update-slice_fusion.12
  372.4 1.4 constant_dynamic-update-slice_fusion.11
  374.4 0.6 constant_dynamic-update-slice_fusion.9
  375.6 0.6 constant_dynamic-update-slice_fusion.7
  377.5 0.6 constant_dynamic-update-slice_fusion.4
  378.1 0.6 constant_dynamic-update-slice_fusion.3
  380.6 5.6 %all-to-all-start.1 = ((bf16[16,1440,16]{1,2,0:T(8,128)(2,1)}), bf16[16,1440,16]{1,2,0:T(8,128)(2,1)S(1)}, u32[]{:S(2)}, u32[]{:S(2)}) async-start(bf16[16,1440,16]{1,2,0:T(8,128)(2,1)} %constant_dynamic-update-slice_fusion), calls=%async_computation.2 | async-start | bytes 1572864 | tf_op jit(solution)/shard_map/all_to_all | solution.py:127
  386.3 21.1 %all-to-all-done.1 = bf16[16,1440,16]{1,2,0:T(8,128)(2,1)S(1)} async-done(((bf16[16,1440,16]{1,2,0:T(8,128)(2,1)}), bf16[16,1440,16]{1,2,0:T(8,128)(2,1)S(1)}, u32[]{:S(2)}, u32[]{:S(2)}) %all-to-all-start.1) | async-done | bytes 737312 | tf_op jit(solution)/shard_map/all_to_all | solution.py:127
  407.4 1.2 fusion.44
  (90 shorter events, 10.5 us)
Async XLA Ops:
  6.5 250.7 %all-reduce.2.cloned.1.call-start = ((), (), s32[]{:S(2)}) async-start(), calls=%async_computation.3 | async-start | bytes 753664 | tf_op jit(solution)/shard_map/psum | solution.py:93
  15.2 1.2 copy-start.2
  49.4 23.2 %collective-permute-start.3 = (f32[4,512,64]{1,2,0:T(8,128)}, f32[4,512,64]{1,2,0:T(8,128)S(1)}, u32[]{:S(2)}, u32[]{:S(2)}) collective-permute-start(f32[4,512,64]{1,2,0:T(8,128)} %fusion.89), channel_id=1, source_target_pairs={{6,0},{0,2},{2,4},{4,6},{7,1},{1,3},{3,5},{5,7},{14,8},{8,10},{10,... | collective-permute-start | bytes 1572872 | tf_op jit(solution)/shard_map/while/body/eval_jaxpr/ppermute | solution.py:13
  52.4 20.1 %collective-permute-start = (bf16[4,512,64]{1,2,0:T(8,128)(2,1)S(1)}, bf16[4,512,64]{1,2,0:T(8,128)(2,1)S(1)}, u32[]{:S(2)}, u32[]{:S(2)}) collective-permute-start(bf16[4,512,64]{1,2,0:T(8,128)(2,1)S(1)} %copy.100), channel_id=1, source_target_pairs={{6,0},{0,2},{2,4},{4,6},{7,1},{1,3},{3,5},{5,7},{14,8},{8,10},{10,... | collective-permute-start | bytes 786440 | tf_op jit(solution)/shard_map/while/body/eval_jaxpr/ppermute | solution.py:13
  54.0 18.5 %collective-permute-start.1 = (f32[4,512]{1,0:T(4,128)S(1)}, f32[4,512]{1,0:T(4,128)S(1)}, u32[]{:S(2)}, u32[]{:S(2)}) collective-permute-start(f32[4,512]{1,0:T(4,128)S(1)} %max.12), channel_id=1, source_target_pairs={{6,0},{0,2},{2,4},{4,6},{7,1},{1,3},{3,5},{5,7},{14,8},{8,10},{10,... | collective-permute-start | bytes 24584 | tf_op jit(solution)/shard_map/while/body/eval_jaxpr/ppermute | solution.py:13
  55.6 17.0 %collective-permute-start.2 = (f32[4,512]{1,0:T(4,128)S(1)}, f32[4,512]{1,0:T(4,128)S(1)}, u32[]{:S(2)}, u32[]{:S(2)}) collective-permute-start(f32[4,512]{1,0:T(4,128)S(1)} %get-tuple-element.468), channel_id=1, source_target_pairs={{6,0},{0,2},{2,4},{4,6},{7,1},{1,3},{3,5},{5,7},{14,8},{8,10},{10,... | collective-permute-start | bytes 24584 | tf_op jit(solution)/shard_map/while/body/eval_jaxpr/ppermute | solution.py:13
  102.8 21.1 %collective-permute-start.3 = (f32[4,512,64]{1,2,0:T(8,128)}, f32[4,512,64]{1,2,0:T(8,128)S(1)}, u32[]{:S(2)}, u32[]{:S(2)}) collective-permute-start(f32[4,512,64]{1,2,0:T(8,128)} %fusion.89), channel_id=1, source_target_pairs={{6,0},{0,2},{2,4},{4,6},{7,1},{1,3},{3,5},{5,7},{14,8},{8,10},{10,... | collective-permute-start | bytes 1572872 | tf_op jit(solution)/shard_map/while/body/eval_jaxpr/ppermute | solution.py:13
  102.8 21.1 %collective-permute-start = (bf16[4,512,64]{1,2,0:T(8,128)(2,1)S(1)}, bf16[4,512,64]{1,2,0:T(8,128)(2,1)S(1)}, u32[]{:S(2)}, u32[]{:S(2)}) collective-permute-start(bf16[4,512,64]{1,2,0:T(8,128)(2,1)S(1)} %copy.100), channel_id=1, source_target_pairs={{6,0},{0,2},{2,4},{4,6},{7,1},{1,3},{3,5},{5,7},{14,8},{8,10},{10,... | collective-permute-start | bytes 786440 | tf_op jit(solution)/shard_map/while/body/eval_jaxpr/ppermute | solution.py:13
  104.1 19.7 %collective-permute-start.1 = (f32[4,512]{1,0:T(4,128)S(1)}, f32[4,512]{1,0:T(4,128)S(1)}, u32[]{:S(2)}, u32[]{:S(2)}) collective-permute-start(f32[4,512]{1,0:T(4,128)S(1)} %max.12), channel_id=1, source_target_pairs={{6,0},{0,2},{2,4},{4,6},{7,1},{1,3},{3,5},{5,7},{14,8},{8,10},{10,... | collective-permute-start | bytes 24584 | tf_op jit(solution)/shard_map/while/body/eval_jaxpr/ppermute | solution.py:13
  105.7 18.2 %collective-permute-start.2 = (f32[4,512]{1,0:T(4,128)S(1)}, f32[4,512]{1,0:T(4,128)S(1)}, u32[]{:S(2)}, u32[]{:S(2)}) collective-permute-start(f32[4,512]{1,0:T(4,128)S(1)} %get-tuple-element.468), channel_id=1, source_target_pairs={{6,0},{0,2},{2,4},{4,6},{7,1},{1,3},{3,5},{5,7},{14,8},{8,10},{10,... | collective-permute-start | bytes 24584 | tf_op jit(solution)/shard_map/while/body/eval_jaxpr/ppermute | solution.py:13
  154.1 20.2 %collective-permute-start.3 = (f32[4,512,64]{1,2,0:T(8,128)}, f32[4,512,64]{1,2,0:T(8,128)S(1)}, u32[]{:S(2)}, u32[]{:S(2)}) collective-permute-start(f32[4,512,64]{1,2,0:T(8,128)} %fusion.89), channel_id=1, source_target_pairs={{6,0},{0,2},{2,4},{4,6},{7,1},{1,3},{3,5},{5,7},{14,8},{8,10},{10,... | collective-permute-start | bytes 1572872 | tf_op jit(solution)/shard_map/while/body/eval_jaxpr/ppermute | solution.py:13
  154.1 20.2 %collective-permute-start = (bf16[4,512,64]{1,2,0:T(8,128)(2,1)S(1)}, bf16[4,512,64]{1,2,0:T(8,128)(2,1)S(1)}, u32[]{:S(2)}, u32[]{:S(2)}) collective-permute-start(bf16[4,512,64]{1,2,0:T(8,128)(2,1)S(1)} %copy.100), channel_id=1, source_target_pairs={{6,0},{0,2},{2,4},{4,6},{7,1},{1,3},{3,5},{5,7},{14,8},{8,10},{10,... | collective-permute-start | bytes 786440 | tf_op jit(solution)/shard_map/while/body/eval_jaxpr/ppermute | solution.py:13
  154.1 20.1 %collective-permute-start.1 = (f32[4,512]{1,0:T(4,128)S(1)}, f32[4,512]{1,0:T(4,128)S(1)}, u32[]{:S(2)}, u32[]{:S(2)}) collective-permute-start(f32[4,512]{1,0:T(4,128)S(1)} %max.12), channel_id=1, source_target_pairs={{6,0},{0,2},{2,4},{4,6},{7,1},{1,3},{3,5},{5,7},{14,8},{8,10},{10,... | collective-permute-start | bytes 24584 | tf_op jit(solution)/shard_map/while/body/eval_jaxpr/ppermute | solution.py:13
  154.9 19.4 %collective-permute-start.2 = (f32[4,512]{1,0:T(4,128)S(1)}, f32[4,512]{1,0:T(4,128)S(1)}, u32[]{:S(2)}, u32[]{:S(2)}) collective-permute-start(f32[4,512]{1,0:T(4,128)S(1)} %get-tuple-element.468), channel_id=1, source_target_pairs={{6,0},{0,2},{2,4},{4,6},{7,1},{1,3},{3,5},{5,7},{14,8},{8,10},{10,... | collective-permute-start | bytes 24584 | tf_op jit(solution)/shard_map/while/body/eval_jaxpr/ppermute | solution.py:13
  204.6 19.4 %collective-permute-start.3 = (f32[4,512,64]{1,2,0:T(8,128)}, f32[4,512,64]{1,2,0:T(8,128)S(1)}, u32[]{:S(2)}, u32[]{:S(2)}) collective-permute-start(f32[4,512,64]{1,2,0:T(8,128)} %fusion.89), channel_id=1, source_target_pairs={{6,0},{0,2},{2,4},{4,6},{7,1},{1,3},{3,5},{5,7},{14,8},{8,10},{10,... | collective-permute-start | bytes 1572872 | tf_op jit(solution)/shard_map/while/body/eval_jaxpr/ppermute | solution.py:13
  204.6 19.4 %collective-permute-start = (bf16[4,512,64]{1,2,0:T(8,128)(2,1)S(1)}, bf16[4,512,64]{1,2,0:T(8,128)(2,1)S(1)}, u32[]{:S(2)}, u32[]{:S(2)}) collective-permute-start(bf16[4,512,64]{1,2,0:T(8,128)(2,1)S(1)} %copy.100), channel_id=1, source_target_pairs={{6,0},{0,2},{2,4},{4,6},{7,1},{1,3},{3,5},{5,7},{14,8},{8,10},{10,... | collective-permute-start | bytes 786440 | tf_op jit(solution)/shard_map/while/body/eval_jaxpr/ppermute | solution.py:13
  204.6 19.3 %collective-permute-start.1 = (f32[4,512]{1,0:T(4,128)S(1)}, f32[4,512]{1,0:T(4,128)S(1)}, u32[]{:S(2)}, u32[]{:S(2)}) collective-permute-start(f32[4,512]{1,0:T(4,128)S(1)} %max.12), channel_id=1, source_target_pairs={{6,0},{0,2},{2,4},{4,6},{7,1},{1,3},{3,5},{5,7},{14,8},{8,10},{10,... | collective-permute-start | bytes 24584 | tf_op jit(solution)/shard_map/while/body/eval_jaxpr/ppermute | solution.py:13
  205.3 18.7 %collective-permute-start.2 = (f32[4,512]{1,0:T(4,128)S(1)}, f32[4,512]{1,0:T(4,128)S(1)}, u32[]{:S(2)}, u32[]{:S(2)}) collective-permute-start(f32[4,512]{1,0:T(4,128)S(1)} %get-tuple-element.468), channel_id=1, source_target_pairs={{6,0},{0,2},{2,4},{4,6},{7,1},{1,3},{3,5},{5,7},{14,8},{8,10},{10,... | collective-permute-start | bytes 24584 | tf_op jit(solution)/shard_map/while/body/eval_jaxpr/ppermute | solution.py:13
  225.4 8.9 %copy-start.4 = (s32[1,64,4]{1,2,0:T(4,128)S(1)}, s32[1,64,4]{1,2,0:T(4,128)}, u32[]{:S(2)}) copy-start(s32[1,64,4]{1,2,0:T(4,128)} %param.23) | copy-start | bytes 3076
  225.4 31.9 %copy-start = (bf16[1,64,2880]{2,1,0:T(8,128)(2,1)S(1)}, bf16[1,64,2880]{2,1,0:T(8,128)(2,1)}, u32[]{:S(2)}) copy-start(bf16[1,64,2880]{2,1,0:T(8,128)(2,1)} %param.15) | copy-start | bytes 1105924
  234.2 25.2 %copy-start.3 = (f32[2880]{0:T(1024)S(1)}, f32[2880]{0:T(1024)}, u32[]{:S(2)}) copy-start(f32[2880]{0:T(1024)} %param.22) | copy-start | bytes 34564
  234.2 115.1 %reduce-scatter.2.cloned.1.call-start = ((), (), s32[]{:S(2)}) async-start(), calls=%async_computation.4 | async-start | bytes 2211840 | tf_op jit(solution)/shard_map/reduce_scatter | solution.py:118
  367.7 18.5 %copy-start.5 = (f32[1,64,4]{1,2,0:T(4,128)S(1)}, f32[1,64,4]{1,2,0:T(4,128)}, u32[]{:S(2)}) copy-start(f32[1,64,4]{1,2,0:T(4,128)} %param.24) | copy-start | bytes 3076
  367.7 39.8 %copy-start.1 = (f32[64,2880]{1,0:T(8,128)S(1)}, f32[64,2880]{1,0:T(8,128)}, u32[]{:S(2)}) copy-start(f32[64,2880]{1,0:T(8,128)} %get-tuple-element.367) | copy-start | bytes 2211844
  380.6 26.8 %all-to-all-start.1 = ((bf16[16,1440,16]{1,2,0:T(8,128)(2,1)}), bf16[16,1440,16]{1,2,0:T(8,128)(2,1)S(1)}, u32[]{:S(2)}, u32[]{:S(2)}) async-start(bf16[16,1440,16]{1,2,0:T(8,128)(2,1)} %constant_dynamic-update-slice_fusion), calls=%async_computation.2 | async-start | bytes 1572864 | tf_op jit(solution)/shard_map/all_to_all | solution.py:127
Sparse Core Ops, SparseCore 0:
  234.3 22.8 all-reduce.1
  326.4 22.8 reduce-scatter.1
